TPU v7x, 256 devices: a whole 4x4x8 slice. The times are simulated.
256 devices in a mesh: side: 2 (over core), group: 16 (over y, z_lo), head: 8 (over x, z_hi).
Axes of the slice: x: 4, y: 4, z: 8 (z_hi: 2, z_lo: 4; z = z_hi * 4 + z_lo), core: 2. Of those that a mesh axis runs over, the one named last changes fastest.
Arguments:
- pool_rows: bfloat16 [2, 6144, 4096], P('side', ('group', 'head')), may hold values from -24 to 24
- pool_weight: bfloat16 [2, 4096, 8192], P('side', 'group', 'head'), as said below
- lengths: int32 [16, 3], replicated, may hold values from 1 to 192, 384 in all within a row
- owner: int32 [16, 3], replicated, may hold values from 0 to 15, as said below
Outputs:
- pool_out: bfloat16 [2, 6144, 4096], P('side', 'group', 'head')
Inputs may be any that keep to these rules, and one draw needn't show every extreme that they name: owner[p, j] is p with the binary digits of m_j flipped, where m_j = owner[0, j] is the same for every p; the m_j differ between slots, and every binary digit below 16 is set in some m_j. So the 3 requests of a prefill group go to different decode groups, and every decode group receives exactly one request for each slot j. `lengths`: each row sums to 384. `pool_weight`: independent normal entries of deviation 1 / sqrt(4096).
All inputs are finite; a program needn't handle non-finite values.
Results may differ from a plain program's by a relative error of at most 0.0061.
Values may be sent and summed in bfloat16 or wider, within the bound.
No kernel may reach another device: no remote copies, remote signals or barrier semaphores. Data moves between devices by JAX's collectives and lax.ppermute only.
A program may use at most 128 MiB of HBM per device.

v0:
```python
import jax
import jax.numpy as jnp
from jax import lax
from jax.sharding import Mesh
from jax.sharding import PartitionSpec as P

HEAD_DIM = 256
GROUP = ("group_0", "group_1")
GROUP_HEAD = ("group_0", "group_1", "head")


def whole_of(value, axes, dim):
    for axis in reversed(axes):
        value = lax.all_gather(value, axis, axis=dim, tiled=True)
    return value


def shifted(value, axis, by):
    count = lax.axis_size(axis)
    pairs = [(i, i + by) for i in range(count) if 0 <= i + by < count]
    return lax.ppermute(value, axis, pairs)


def swapped(block, axis, bit):
    count = lax.axis_size(axis)
    route = []
    for low in range(count):
        high = low | 1 << bit
        if high != low and high < count:
            route += [(low, high), (high, low)]
    return lax.ppermute(block, axis, route)


def attend_direct(query_rows, memory_rows, count, wide, scale):
    maxlen = memory_rows.shape[0]
    rows = query_rows.shape[0]
    heads_dev = wide // HEAD_DIM
    queries = query_rows.reshape(rows, heads_dev, HEAD_DIM)
    key_rows = memory_rows[:, :wide].reshape(maxlen, heads_dev, HEAD_DIM)
    value_rows = memory_rows[:, wide:].reshape(maxlen, heads_dev, HEAD_DIM)
    scores = (
        jnp.einsum("qeh,keh->eqk", queries, key_rows, preferred_element_type=jnp.float32) * scale
    )
    valid = jnp.arange(maxlen, dtype=jnp.int32) < count
    scores = jnp.where(valid[None, None, :], scores, -1e30)
    peak = jnp.max(scores, axis=-1, keepdims=True)
    expo = jnp.where(valid[None, None, :], jnp.exp(scores - peak), 0.0)
    total = jnp.sum(expo, axis=-1)
    mixed = jnp.einsum(
        "eqk,keh->eqh", expo.astype(jnp.bfloat16), value_rows, preferred_element_type=jnp.float32
    )
    mixed = mixed / total[:, :, None]
    return jnp.transpose(mixed, (1, 0, 2)).reshape(rows, wide)


def on_device(pool_rows, pool_weight, lengths, owner):
    side_index = lax.axis_index("side")
    group_index = lax.axis_index(GROUP)
    requests = lengths.shape[1]
    gathered = lax.all_gather(pool_rows[0], "head", axis=0, tiled=True)
    weight = whole_of(pool_weight[0], GROUP, 0)
    mem_g = gathered.shape[0]
    wide = weight.shape[1] // 2
    q_req = mem_g // requests
    maxlen = mem_g // 2
    scale = 1.0 / HEAD_DIM**0.5
    cached = jnp.dot(gathered, weight, preferred_element_type=jnp.float32).astype(jnp.bfloat16)
    queries = cached[:, :wide]
    starts = jnp.cumsum(lengths, axis=1) - lengths
    groups = jnp.arange(lengths.shape[0], dtype=jnp.int32)
    sources, begins, counts = ([], [], [])
    for slot in range(requests):
        hit = owner[:, slot] == group_index
        sources.append(jnp.sum(jnp.where(hit, groups, 0)))
        begins.append(jnp.sum(jnp.where(hit, starts[:, slot], 0)))
        counts.append(jnp.sum(jnp.where(hit, lengths[:, slot], 0)))
    moved = shifted(cached, "side", 1)
    padded = jnp.concatenate([moved, jnp.zeros((maxlen, moved.shape[1]), jnp.bfloat16)], axis=0)
    own_starts = lax.dynamic_index_in_dim(starts, group_index, 0, keepdims=False)
    holding = jnp.stack(
        [lax.dynamic_slice_in_dim(padded, own_starts[slot], maxlen, 0) for slot in range(requests)],
        axis=0,
    )
    flips = owner[0]
    for digit in range(lax.axis_size(GROUP).bit_length() - 1):
        partner = swapped(holding, GROUP, digit)
        moving = jnp.bitwise_and(jnp.right_shift(flips, digit), 1) == 1
        holding = jnp.where(moving[:, None, None], partner, holding)
    pieces = []
    for slot in range(requests):
        query_rows = queries[slot * q_req : (slot + 1) * q_req]
        pieces.append(attend_direct(query_rows, holding[slot], counts[slot], wide, scale))
    attended = jnp.concatenate(pieces, axis=0).astype(jnp.bfloat16)
    partial_out = lax.dot_general(
        attended, weight[:, wide:], (((1,), (1,)), ((), ())), preferred_element_type=jnp.float32
    )
    decoded = lax.psum_scatter(partial_out, "head", scatter_dimension=1, tiled=True).astype(
        jnp.bfloat16
    )
    result = jnp.where(side_index == 0, cached[:, :wide], decoded)
    return result[None]


def solution(mesh):
    torus = Mesh(
        mesh.devices.reshape(mesh.shape["side"], 4, 4, mesh.shape["head"]),
        ("side", "group_0", "group_1", "head"),
    )
    in_specs = (P("side", GROUP_HEAD, None), P("side", GROUP, "head"), P(), P())
    out_specs = P("side", GROUP, "head")
    return jax.shard_map(
        on_device, mesh=torus, in_specs=in_specs, out_specs=out_specs, check_vma=False
    )
```

profile of v0, /device:TPU:8, one launch (start us, length us, event | category | flops | bytes accessed | tf_op | source)
XLA Modules:
  0.0 563.7 jit_solution(15055022247647864078)
XLA Ops:
  6.5 0.7 all-gather.9.cloned.1.call-update
  7.3 0.7 all-gather.7.cloned.1.call-update
  8.1 54.0 %all-gather.9.cloned.1.call-done = bf16[1,1024,1024]{2,1,0:T(8,128)(2,1)} async-done(((bf16[1,256,1024]{2,1,0:T(8,128)(2,1)}), bf16[1,1024,1024]{2,1,0:T(8,128)(2,1)}) %all-gather.9.cloned.1.call-update) | async-done | bytes 2097168 | tf_op jit(solution)/shard_map/all_gather | solution.py:14
  62.1 93.6 %all-gather.7.cloned.1.call-done = bf16[1,384,4096]{2,1,0:T(8,128)(2,1)} async-done(((bf16[1,48,4096]{2,1,0:T(8,128)(2,1)}), bf16[1,384,4096]{2,1,0:T(8,128)(2,1)}) %all-gather.7.cloned.1.call-update) | async-done | bytes 3145744 | tf_op jit(solution)/shard_map/all_gather | solution.py:60
  155.7 82.9 %all-gather.11.cloned.1.call-done = bf16[1,4096,1024]{2,1,0:T(8,128)(2,1)} async-done(((bf16[1,1024,1024]{2,1,0:T(8,128)(2,1)}), bf16[1,4096,1024]{2,1,0:T(8,128)(2,1)}) %all-gather.11.cloned.1.call-update) | async-done | bytes 8388624 | tf_op jit(solution)/shard_map/all_gather | solution.py:14
  238.6 7.7 %fusion.7 = bf16[384,1024]{1,0:T(8,128)(2,1)S(1)} fusion(bf16[1,384,4096]{2,1,0:T(8,128)(2,1)} %all-gather.7.cloned.1.call-done, bf16[1,4096,1024]{2,1,0:T(8,128)(2,1)} %all-gather.11.cloned.1.call-done), kind=kOutput, calls=%fused_computation.7 | convolution fusion | flops 3221618688 | bytes 12320768 | tf_op jit(solution)/shard_map/dot_general | solution.py:67
  246.4 1.6 collective-permute-start
  248.1 0.5 fusion.77
  254.2 0.8 fusion.28
  255.2 1.6 collective-permute-start.1
  256.9 25.5 %collective-permute-done.1 = bf16[3,192,1024]{2,1,0:T(8,128)(2,1)S(1)} collective-permute-done((bf16[3,192,1024]{2,1,0:T(8,128)(2,1)S(1)}, bf16[3,192,1024]{2,1,0:T(8,128)(2,1)S(1)}, u32[]{:S(2)}, u32[]{:S(2)}) %collective-permute-start.1) | collective-permute-done | bytes 1179680 | tf_op jit(solution)/shard_map/ppermute | solution.py:31
  282.7 2.6 collective-permute-start.2
  285.3 50.0 %collective-permute-done.2 = bf16[3,192,1024]{2,1,0:T(8,128)(2,1)S(1)} collective-permute-done((bf16[3,192,1024]{2,1,0:T(8,128)(2,1)S(1)}, bf16[3,192,1024]{2,1,0:T(8,128)(2,1)S(1)}, u32[]{:S(2)}, u32[]{:S(2)}) %collective-permute-start.2) | collective-permute-done | bytes 1179680 | tf_op jit(solution)/shard_map/ppermute | solution.py:31
  335.5 0.7 collective-permute-start.3
  336.2 26.3 %collective-permute-done.3 = bf16[3,192,1024]{2,1,0:T(8,128)(2,1)S(1)} collective-permute-done((bf16[3,192,1024]{2,1,0:T(8,128)(2,1)S(1)}, bf16[3,192,1024]{2,1,0:T(8,128)(2,1)S(1)}, u32[]{:S(2)}, u32[]{:S(2)}) %collective-permute-start.3) | collective-permute-done | bytes 1179680 | tf_op jit(solution)/shard_map/ppermute | solution.py:31
  362.7 1.4 collective-permute-start.4
  364.1 0.7 fusion.65
  364.8 0.6 iota_compare_fusion.2
  365.5 1.2 iota_compare_fusion
  366.7 23.7 %collective-permute-done.4 = bf16[3,192,1024]{2,1,0:T(8,128)(2,1)S(1)} collective-permute-done((bf16[3,192,1024]{2,1,0:T(8,128)(2,1)S(1)}, bf16[3,192,1024]{2,1,0:T(8,128)(2,1)S(1)}, u32[]{:S(2)}, u32[]{:S(2)}) %collective-permute-start.4) | collective-permute-done | bytes 1179680 | tf_op jit(solution)/shard_map/ppermute | solution.py:31
  391.8 0.3 fusion.17
  393.0 6.8 %fusion.3 = f32[384,4096]{1,0:T(8,128)} fusion(bf16[4096,1024]{1,0:T(8,128)(2,1)} %bitcast.91, bf16[128,512]{0,1:T(8,128)(2,1)S(1)} %bitcast.94, bf16[128,512]{0,1:T(8,128)(2,1)S(1)} %bitcast.93, bf16[128,512]{0,1:T(8,128)(2,1)S(1)} %bitcast.92), kind=kOutput, calls=%fused_computation.3 | convolution fusion | flops 1611792384 | bytes 10878976 | tf_op jit(solution)/shard_map/dot_general | solution.py:94
  399.9 155.4 %reduce-scatter.2.cloned.1.call-done = f32[384,512]{1,0:T(8,128)} async-done(((f32[384,4096]{1,0:T(8,128)}), f32[384,512]{1,0:T(8,128)}) %reduce-scatter.2.cloned.1.call-update) | async-done | bytes 786448 | tf_op jit(solution)/shard_map/reduce_scatter | solution.py:97
  555.3 1.9 fusion.31
  (35 shorter events, 3.5 us)
Async XLA Ops:
  6.5 55.5 %all-gather.9.cloned.1.call-start = ((), (), s32[]{:S(2)}) async-start(), calls=%async_computation.3 | async-start | bytes 2621440 | tf_op jit(solution)/shard_map/all_gather | solution.py:14
  7.3 148.5 %all-gather.7.cloned.1.call-start = ((), (), s32[]{:S(2)}) async-start(), calls=%async_computation.2 | async-start | bytes 3538944 | tf_op jit(solution)/shard_map/all_gather | solution.py:60
  8.0 230.6 %all-gather.11.cloned.1.call-start = ((), (), s32[]{:S(2)}) async-start(), calls=%async_computation.4 | async-start | bytes 10485760 | tf_op jit(solution)/shard_map/all_gather | solution.py:14
  62.0 186.0 %copy-start = (s32[16,3]{0,1:T(4,128)S(1)}, s32[16,3]{0,1:T(4,128)}, u32[]{:S(2)}) copy-start(s32[16,3]{0,1:T(4,128)} %param.6) | copy-start | bytes 580
  62.1 493.2 %reduce-scatter.2.cloned.1.call-start = ((), (), s32[]{:S(2)}) async-start(), calls=%async_computation.1 | async-start | bytes 7077888 | tf_op jit(solution)/shard_map/reduce_scatter | solution.py:97
  246.4 7.8 %collective-permute-start = (bf16[384,1024]{1,0:T(8,128)(2,1)S(1)}, bf16[384,1024]{1,0:T(8,128)(2,1)S(1)}, u32[]{:S(2)}, u32[]{:S(2)}) collective-permute-start(bf16[384,1024]{1,0:T(8,128)(2,1)S(1)} %fusion.7), channel_id=1, source_target_pairs={{0,128},{1,129},{2,130},{3,131},{4,132},{5,133},{6,134},{7,135},{8... | collective-permute-start | bytes 2359304 | tf_op jit(solution)/shard_map/ppermute | solution.py:21
  255.0 1.8 copy-start.1
  255.2 27.3 %collective-permute-start.1 = (bf16[3,192,1024]{2,1,0:T(8,128)(2,1)S(1)}, bf16[3,192,1024]{2,1,0:T(8,128)(2,1)S(1)}, u32[]{:S(2)}, u32[]{:S(2)}) collective-permute-start(bf16[3,192,1024]{2,1,0:T(8,128)(2,1)S(1)} %pad_maximum_fusion), channel_id=1, source_target_pairs={{0,8},{8,0},{16,24},{24,16},{32,40},{40,32},{48,56},{56,48},{64,72... | collective-permute-start | bytes 3538952 | tf_op jit(solution)/shard_map/ppermute | solution.py:31
  282.7 52.6 %collective-permute-start.2 = (bf16[3,192,1024]{2,1,0:T(8,128)(2,1)S(1)}, bf16[3,192,1024]{2,1,0:T(8,128)(2,1)S(1)}, u32[]{:S(2)}, u32[]{:S(2)}) collective-permute-start(bf16[3,192,1024]{2,1,0:T(8,128)(2,1)S(1)} %broadcast_select_fusion), channel_id=1, source_target_pairs={{0,16},{16,0},{8,24},{24,8},{32,48},{48,32},{40,56},{56,40},{64,80... | collective-permute-start | bytes 3538952 | tf_op jit(solution)/shard_map/ppermute | solution.py:31
  335.5 27.0 %collective-permute-start.3 = (bf16[3,192,1024]{2,1,0:T(8,128)(2,1)S(1)}, bf16[3,192,1024]{2,1,0:T(8,128)(2,1)S(1)}, u32[]{:S(2)}, u32[]{:S(2)}) collective-permute-start(bf16[3,192,1024]{2,1,0:T(8,128)(2,1)S(1)} %broadcast_select_fusion.1), channel_id=1, source_target_pairs={{0,32},{32,0},{8,40},{40,8},{16,48},{48,16},{24,56},{56,24},{64,96... | collective-permute-start | bytes 3538952 | tf_op jit(solution)/shard_map/ppermute | solution.py:31
  362.7 27.6 %collective-permute-start.4 = (bf16[3,192,1024]{2,1,0:T(8,128)(2,1)S(1)}, bf16[3,192,1024]{2,1,0:T(8,128)(2,1)S(1)}, u32[]{:S(2)}, u32[]{:S(2)}) collective-permute-start(bf16[3,192,1024]{2,1,0:T(8,128)(2,1)S(1)} %broadcast_select_fusion.2), channel_id=1, source_target_pairs={{0,64},{64,0},{8,72},{72,8},{16,80},{80,16},{24,88},{88,24},{32,96... | collective-permute-start | bytes 3538952 | tf_op jit(solution)/shard_map/ppermute | solution.py:31
Sparse Core Ops, SparseCore 0:
  9.1 52.8 all-gather.8
  64.6 91.0 all-gather.6
  157.5 81.0 all-gather.10
  400.0 155.2 reduce-scatter.1
where the time goes:
time: 564 us
  waiting for transfers between devices  513 us (91%)
  between operations  18.8 us (3%)
  matrix products  16.1 us (3%)
  starting transfers between devices  8.07 us (1%)
  other arithmetic  5.96 us (1%)
    reduce_scatter x1, waiting for transfers between devices, on_device(): lax.psum_scatter(partial_out, 'head', scatter_dimension=1, tiled=True)  155 us
    all_gather x2, waiting for transfers between devices, whole_of(): value = lax.all_gather(value, axis, axis=dim, tiled=True)  137 us
    ppermute x4, waiting for transfers between devices, swapped(): return lax.ppermute(block, axis, route)  125 us
    all_gather x1, waiting for transfers between devices, on_device(): gathered = lax.all_gather(pool_rows[0], 'head', axis=0, tiled=True)  93.6 us
  transfers between devices with their start and end apart: 9, of which 8 were waited for; matrix products, arithmetic and copies ran while one was open for 1% of the time, Pallas kernels for 0%

commit v1 on v0

--- a/solution.py
+++ b/solution.py
@@ -57,7 +57,11 @@
     side_index = lax.axis_index("side")
     group_index = lax.axis_index(GROUP)
     requests = lengths.shape[1]
-    gathered = lax.all_gather(pool_rows[0], "head", axis=0, tiled=True)
+    x = pool_rows[0]
+    size = lax.axis_size("head")
+    parts = jnp.stack([x for _ in range(size)])
+    parts = lax.all_to_all(parts, "head", split_axis=0, concat_axis=0)
+    gathered = jnp.concatenate(parts, axis=0)
     weight = whole_of(pool_weight[0], GROUP, 0)
     mem_g = gathered.shape[0]
     wide = weight.shape[1] // 2

time: 564 us -> 474 us (0.84)
  waiting for transfers between devices: 513 us -> 340 us
  blocking collectives: 0 us -> 82.3 us
    all_gather x1 -> x0, waiting for transfers between devices: 93.6 us -> none  [on_device(): gathered = lax.all_gather(pool_rows[0], 'head', axis=0, tiled=True)]
    all_to_all x0 -> x1, blocking collectives: none -> 82.3 us  [on_device(): parts = lax.all_to_all(parts, 'head', split_axis=0, concat_axis=0)]
    all_gather x2, waiting for transfers between devices: 137 us -> 59.1 us  [whole_of(): value = lax.all_gather(value, axis, axis=dim, tiled=True)]
  transfers between devices with their start and end apart: 9 -> 8, of which waited for: 8 -> 7; matrix products, arithmetic and copies ran while one was open for 1% -> 1% of each run, Pallas kernels for 0% -> 0%
where the time goes in v1:
time: 474 us; the launch traced here: 473 us
  waiting for transfers between devices  340 us (72%)
  blocking collectives  82.3 us (17%)
  between operations  18.8 us (4%)
  matrix products  15.1 us (3%)
  starting transfers between devices  8.01 us (2%)
  other arithmetic  6.08 us (1%)
    reduce_scatter x1, waiting for transfers between devices, on_device(): lax.psum_scatter(partial_out, 'head', scatter_dimension=1, tiled=True)  155 us
    ppermute x4, waiting for transfers between devices, swapped(): return lax.ppermute(block, axis, route)  124 us
    all_to_all x1, blocking collectives, on_device(): parts = lax.all_to_all(parts, 'head', split_axis=0, concat_axis=0)  82.3 us
    all_gather x2, waiting for transfers between devices, whole_of(): value = lax.all_gather(value, axis, axis=dim, tiled=True)  59.1 us
  transfers between devices with their start and end apart: 8, of which 7 were waited for; matrix products, arithmetic and copies ran while one was open for 1% of the time, Pallas kernels for 0%

profile of v1, /device:TPU:8, one launch (start us, length us, event | category | flops | bytes accessed | tf_op | source)
XLA Modules:
  0.0 473.4 jit_solution(6060865188185372267)
XLA Ops:
  6.5 0.7 all-gather.5.cloned.1.call-update
  7.3 54.7 %all-gather.5.cloned.1.call-done = bf16[1,1024,1024]{2,1,0:T(8,128)(2,1)} async-done(((bf16[1,256,1024]{2,1,0:T(8,128)(2,1)}), bf16[1,1024,1024]{2,1,0:T(8,128)(2,1)}) %all-gather.5.cloned.1.call-update) | async-done | bytes 2097168 | tf_op jit(solution)/shard_map/all_gather | solution.py:14
  62.1 0.4 stack.15
  62.5 82.3 %all_to_all.5 = bf16[8,48,4096]{2,1,0:T(8,128)(2,1)S(1)} all-to-all(bf16[8,48,4096]{2,1,0:T(8,128)(2,1)S(1)} %stack.15), channel_id=1, replica_groups=mesh['side'=2,'group_0'=4,'group_1'=4,'head'=8] {'head'}, dimensions={0} | all-to-all | bytes 6291456 | tf_op jit(solution)/shard_map/all_to_all | solution.py:63
  144.7 4.3 all-gather.7.cloned.1.call-done
  149.1 6.8 %convolution_convert_fusion = bf16[384,1024]{1,0:T(8,128)(2,1)} fusion(bf16[384,4096]{1,0:T(8,128)(2,1)S(1)} %bitcast.89, bf16[1,4096,1024]{2,1,0:T(8,128)(2,1)} %all-gather.7.cloned.1.call-done), kind=kOutput, calls=%fused_computation.5 | convolution fusion | flops 3221618688 | bytes 12320768 | tf_op jit(solution)/shard_map/dot_general | solution.py:71
  155.9 1.6 collective-permute-start
  157.6 0.5 fusion.72
  163.7 0.8 fusion.23
  164.6 1.6 collective-permute-start.1
  166.4 25.5 %collective-permute-done.1 = bf16[3,192,1024]{2,1,0:T(8,128)(2,1)S(1)} collective-permute-done((bf16[3,192,1024]{2,1,0:T(8,128)(2,1)S(1)}, bf16[3,192,1024]{2,1,0:T(8,128)(2,1)S(1)}, u32[]{:S(2)}, u32[]{:S(2)}) %collective-permute-start.1) | collective-permute-done | bytes 1179680 | tf_op jit(solution)/shard_map/ppermute | solution.py:31
  192.2 2.6 collective-permute-start.2
  194.8 50.0 %collective-permute-done.2 = bf16[3,192,1024]{2,1,0:T(8,128)(2,1)S(1)} collective-permute-done((bf16[3,192,1024]{2,1,0:T(8,128)(2,1)S(1)}, bf16[3,192,1024]{2,1,0:T(8,128)(2,1)S(1)}, u32[]{:S(2)}, u32[]{:S(2)}) %collective-permute-start.2) | collective-permute-done | bytes 1179680 | tf_op jit(solution)/shard_map/ppermute | solution.py:31
  245.0 0.7 collective-permute-start.3
  245.7 26.3 %collective-permute-done.3 = bf16[3,192,1024]{2,1,0:T(8,128)(2,1)S(1)} collective-permute-done((bf16[3,192,1024]{2,1,0:T(8,128)(2,1)S(1)}, bf16[3,192,1024]{2,1,0:T(8,128)(2,1)S(1)}, u32[]{:S(2)}, u32[]{:S(2)}) %collective-permute-start.3) | collective-permute-done | bytes 1179680 | tf_op jit(solution)/shard_map/ppermute | solution.py:31
  272.2 1.4 collective-permute-start.4
  273.6 0.7 fusion.60
  274.3 0.6 iota_compare_fusion.2
  274.9 1.2 iota_compare_fusion
  276.1 1.1 fusion.68
  277.2 22.6 %collective-permute-done.4 = bf16[3,192,1024]{2,1,0:T(8,128)(2,1)S(1)} collective-permute-done((bf16[3,192,1024]{2,1,0:T(8,128)(2,1)S(1)}, bf16[3,192,1024]{2,1,0:T(8,128)(2,1)S(1)}, u32[]{:S(2)}, u32[]{:S(2)}) %collective-permute-start.4) | collective-permute-done | bytes 1179680 | tf_op jit(solution)/shard_map/ppermute | solution.py:31
  302.5 6.8 %fusion.3 = f32[384,4096]{1,0:T(8,128)} fusion(bf16[4096,1024]{1,0:T(8,128)(2,1)} %bitcast.90, bf16[128,512]{0,1:T(8,128)(2,1)S(1)} %bitcast.93, bf16[128,512]{0,1:T(8,128)(2,1)S(1)} %bitcast.92, bf16[128,512]{0,1:T(8,128)(2,1)S(1)} %bitcast.91), kind=kOutput, calls=%fused_computation.3 | convolution fusion | flops 1611792384 | bytes 10878976 | tf_op jit(solution)/shard_map/dot_general | solution.py:98
  309.3 155.5 %reduce-scatter.2.cloned.1.call-done = f32[384,512]{1,0:T(8,128)} async-done(((f32[384,4096]{1,0:T(8,128)}), f32[384,512]{1,0:T(8,128)}) %reduce-scatter.2.cloned.1.call-update) | async-done | bytes 786448 | tf_op jit(solution)/shard_map/reduce_scatter | solution.py:101
  464.8 2.1 fusion.26
  (36 shorter events, 3.8 us)
Async XLA Ops:
  6.5 55.5 %all-gather.5.cloned.1.call-start = ((), (), s32[]{:S(2)}) async-start(), calls=%async_computation.3 | async-start | bytes 2621440 | tf_op jit(solution)/shard_map/all_gather | solution.py:14
  7.3 54.8 %copy-start = (bf16[1,48,4096]{2,1,0:T(8,128)(2,1)S(1)}, bf16[1,48,4096]{2,1,0:T(8,128)(2,1)}, u32[]{:S(2)}) copy-start(bf16[1,48,4096]{2,1,0:T(8,128)(2,1)} %param.4) | copy-start | bytes 1179652
  7.3 141.8 %all-gather.7.cloned.1.call-start = ((), (), s32[]{:S(2)}) async-start(), calls=%async_computation.4 | async-start | bytes 10485760 | tf_op jit(solution)/shard_map/all_gather | solution.py:14
  62.0 402.7 %reduce-scatter.2.cloned.1.call-start = ((), (), s32[]{:S(2)}) async-start(), calls=%async_computation.2 | async-start | bytes 7077888 | tf_op jit(solution)/shard_map/reduce_scatter | solution.py:101
  149.1 8.4 %copy-start.1 = (s32[16,3]{0,1:T(4,128)S(1)}, s32[16,3]{0,1:T(4,128)}, u32[]{:S(2)}) copy-start(s32[16,3]{0,1:T(4,128)} %param.6) | copy-start | bytes 580
  155.9 7.8 %collective-permute-start = (bf16[384,1024]{1,0:T(8,128)(2,1)}, bf16[384,1024]{1,0:T(8,128)(2,1)S(1)}, u32[]{:S(2)}, u32[]{:S(2)}) collective-permute-start(bf16[384,1024]{1,0:T(8,128)(2,1)} %convolution_convert_fusion), channel_id=1, source_target_pairs={{0,128},{1,129},{2,130},{3,131},{4,132},{5,133},{6,134},{7,135},{8... | collective-permute-start | bytes 2359304 | tf_op jit(solution)/shard_map/ppermute | solution.py:21
  164.5 1.8 copy-start.2
  164.6 27.3 %collective-permute-start.1 = (bf16[3,192,1024]{2,1,0:T(8,128)(2,1)S(1)}, bf16[3,192,1024]{2,1,0:T(8,128)(2,1)S(1)}, u32[]{:S(2)}, u32[]{:S(2)}) collective-permute-start(bf16[3,192,1024]{2,1,0:T(8,128)(2,1)S(1)} %pad_maximum_fusion), channel_id=1, source_target_pairs={{0,8},{8,0},{16,24},{24,16},{32,40},{40,32},{48,56},{56,48},{64,72... | collective-permute-start | bytes 3538952 | tf_op jit(solution)/shard_map/ppermute | solution.py:31
  192.2 52.6 %collective-permute-start.2 = (bf16[3,192,1024]{2,1,0:T(8,128)(2,1)S(1)}, bf16[3,192,1024]{2,1,0:T(8,128)(2,1)S(1)}, u32[]{:S(2)}, u32[]{:S(2)}) collective-permute-start(bf16[3,192,1024]{2,1,0:T(8,128)(2,1)S(1)} %broadcast_select_fusion), channel_id=1, source_target_pairs={{0,16},{16,0},{8,24},{24,8},{32,48},{48,32},{40,56},{56,40},{64,80... | collective-permute-start | bytes 3538952 | tf_op jit(solution)/shard_map/ppermute | solution.py:31
  245.0 27.0 %collective-permute-start.3 = (bf16[3,192,1024]{2,1,0:T(8,128)(2,1)S(1)}, bf16[3,192,1024]{2,1,0:T(8,128)(2,1)S(1)}, u32[]{:S(2)}, u32[]{:S(2)}) collective-permute-start(bf16[3,192,1024]{2,1,0:T(8,128)(2,1)S(1)} %broadcast_select_fusion.1), channel_id=1, source_target_pairs={{0,32},{32,0},{8,40},{40,8},{16,48},{48,16},{24,56},{56,24},{64,96... | collective-permute-start | bytes 3538952 | tf_op jit(solution)/shard_map/ppermute | solution.py:31
  272.2 27.6 %collective-permute-start.4 = (bf16[3,192,1024]{2,1,0:T(8,128)(2,1)S(1)}, bf16[3,192,1024]{2,1,0:T(8,128)(2,1)S(1)}, u32[]{:S(2)}, u32[]{:S(2)}) collective-permute-start(bf16[3,192,1024]{2,1,0:T(8,128)(2,1)S(1)} %broadcast_select_fusion.2), channel_id=1, source_target_pairs={{0,64},{64,0},{8,72},{72,8},{16,80},{80,16},{24,88},{88,24},{32,96... | collective-permute-start | bytes 3538952 | tf_op jit(solution)/shard_map/ppermute | solution.py:31
Sparse Core Ops, SparseCore 0:
  9.1 52.8 all-gather.4
  63.8 85.1 all-gather.6
  309.4 155.3 reduce-scatter.1
